TPU v7x, 32 devices: a whole 2x2x4 slice. The times are simulated.
32 devices in a mesh: dp: 8 (over z, core), tensor: 4 (over y, x).
Axes of the slice: x: 2, y: 2, z: 4, core: 2. Of those that a mesh axis runs over, the one named last changes fastest.
Arguments:
- latents: bfloat16 [88, 256, 640], P('dp', 'tensor'), may hold values from -6 to 6
- cotangent: bfloat16 [88, 256, 640], P('dp', 'tensor'), may hold values from -6 to 6
- trunc_steps: int32 [8], replicated, may hold values from 30 to 40, as said below
- timesteps: int32 [88], replicated, may hold values from 100 to 900
- tile_map: int32 [88], replicated, may hold values from 0 to 87, as said below
- gain: float32 [640], replicated, may hold values from 0.5 to 1.5
- w_value: bfloat16 [640, 2560], P(None, 'tensor'), may hold values from -0.25 to 0.25
- w_gate: bfloat16 [640, 2560], P(None, 'tensor'), may hold values from -0.25 to 0.25
- w_out: bfloat16 [640, 2560], P(None, 'tensor'), may hold values from -0.125 to 0.125
Outputs:
- placed_grad: bfloat16 [88, 256, 640], P('dp', 'tensor')
- grad_value: float32 [640, 2560], P('dp', 'tensor')
- grad_gate: float32 [640, 2560], P('dp', 'tensor')
- grad_out_proj: float32 [640, 2560], P('dp', 'tensor')
- grad_gain: float32 [640], replicated
Inputs may be any that keep to these rules, and one draw needn't show every extreme that they name: trunc_steps lies in 30 to 40, so a prompt has 1 to 11 live slots, its lowest ones. tile_map is a permutation of 0 to 87. Output slots g * 11 to g * 11 + 10 form group g; the live items go to the lowest slots of the groups, and each group receives the floor or the ceiling of (number of live items) / 8 of them.
All inputs are finite; a program needn't handle non-finite values.
Results may differ from a plain program's by a relative error of at most 0.0068.
Values may be sent and summed in bfloat16 or wider, within the bound.
A program may use at most 64 MiB of HBM per device.

v0:
```python
import jax
import jax.numpy as jnp
from jax import lax
from jax.sharding import PartitionSpec as P

eps = 1e-05


def alpha_bars():
    betas = jnp.linspace(0.00085**0.5, 0.012**0.5, 1000, dtype=jnp.float32) ** 2
    return jnp.exp(jnp.cumsum(jnp.log1p(-betas)))


def gelu_parts(inputs):
    cdf = 0.5 * (1.0 + lax.erf(inputs * 0.7071067811865476))
    density = jnp.exp(-0.5 * inputs * inputs) * 0.3989422804014327
    return (inputs * cdf, cdf + inputs * density)


def norm_backward(d_normed, grad_part, hat_part, inv_part, gain):
    d_hat = d_normed * gain
    input_grad = grad_part.astype(jnp.float32) + inv_part * (
        d_hat
        - jnp.mean(d_hat, axis=-1, keepdims=True)
        - hat_part * jnp.mean(d_hat * hat_part, axis=-1, keepdims=True)
    )
    gain_local = jnp.sum(d_normed * hat_part, axis=(0, 1))
    return (input_grad, gain_local)


def tile_backward(tiles, cot_tiles, slot_times, live_count, gain, w_value, w_gate, w_out):
    full_x, full_cot = (
        lax.all_gather(tiles, "tensor", axis=1, tiled=True),
        lax.all_gather(cot_tiles, "tensor", axis=1, tiled=True),
    )
    width = full_x.shape[2]
    local_rows = tiles.shape[1]
    inner = w_value.shape[1]
    slot_total = full_x.shape[0]
    table = alpha_bars()
    picked = jnp.sum(
        jnp.where(
            slot_times[:, None] == jnp.arange(1000, dtype=jnp.int32)[None, :], table[None, :], 0.0
        ),
        axis=1,
    )
    noise_scale = jnp.sqrt(1.0 - picked)
    x_float = full_x.astype(jnp.float32)
    row_mean = jnp.mean(x_float, axis=-1, keepdims=True)
    centred = x_float - row_mean
    row_var = jnp.mean(centred * centred, axis=-1, keepdims=True)
    inv_std = lax.rsqrt(row_var + eps)
    x_hat = centred * inv_std
    normed = (x_hat * gain).astype(jnp.bfloat16)
    grad_tile = (full_cot.astype(jnp.float32) * noise_scale[:, None, None]).astype(jnp.bfloat16)
    first_dims = (((0,), (0,)), ((), ()))
    last_dims = (((1,), (1,)), ((), ()))

    def one_slot(slot_idx, carry):
        acc_wv, acc_wg, acc_wo, normed_buf = carry
        norm_tile = lax.dynamic_index_in_dim(normed, slot_idx, 0, keepdims=False)
        grad_one = lax.dynamic_index_in_dim(grad_tile, slot_idx, 0, keepdims=False)
        values_proj = jnp.dot(norm_tile, w_value, preferred_element_type=jnp.float32)
        gate_proj = jnp.dot(norm_tile, w_gate, preferred_element_type=jnp.float32)
        gelu_gate, gelu_slope = gelu_parts(gate_proj)
        hidden = (values_proj * gelu_gate).astype(jnp.bfloat16)
        d_hidden = jnp.dot(grad_one, w_out, preferred_element_type=jnp.float32)
        d_value = (d_hidden * gelu_gate).astype(jnp.bfloat16)
        d_gate = (d_hidden * values_proj * gelu_slope).astype(jnp.bfloat16)
        acc_wv = acc_wv + lax.dot_general(
            norm_tile, d_value, first_dims, preferred_element_type=jnp.float32
        )
        acc_wg = acc_wg + lax.dot_general(
            norm_tile, d_gate, first_dims, preferred_element_type=jnp.float32
        )
        acc_wo = acc_wo + lax.dot_general(
            grad_one, hidden, first_dims, preferred_element_type=jnp.float32
        )
        d_normed = lax.dot_general(d_value, w_value, last_dims, preferred_element_type=jnp.float32)
        d_normed = d_normed + lax.dot_general(
            d_gate, w_gate, last_dims, preferred_element_type=jnp.float32
        )
        normed_buf = lax.dynamic_update_index_in_dim(normed_buf, d_normed, slot_idx, 0)
        return (acc_wv, acc_wg, acc_wo, normed_buf)

    zero_w = jnp.zeros((width, inner), jnp.float32)
    init = (zero_w, zero_w, zero_w, jnp.zeros(full_x.shape, jnp.float32))
    acc_wv, acc_wg, acc_wo, normed_buf = lax.fori_loop(0, live_count, one_slot, init)
    offset = lax.axis_index("tensor") * local_rows
    hat_part = lax.dynamic_slice_in_dim(x_hat, offset, local_rows, 1)
    inv_part = lax.dynamic_slice_in_dim(inv_std, offset, local_rows, 1)
    grad_part = lax.dynamic_slice_in_dim(grad_tile, offset, local_rows, 1)
    slot_live = (jnp.arange(slot_total, dtype=jnp.int32) < live_count)[:, None, None]
    d_normed = lax.psum_scatter(normed_buf, "tensor", scatter_dimension=1, tiled=True)
    input_grad, gain_local = norm_backward(d_normed, grad_part, hat_part, inv_part, gain)
    input_grad = jnp.where(slot_live, input_grad, 0.0).astype(jnp.bfloat16)
    return (input_grad, (acc_wv, acc_wg, acc_wo), gain_local)


def per_device(latents, cotangent, trunc_steps, timesteps, tile_map, gain, w_value, w_gate, w_out):
    slot_total = latents.shape[0]
    total = tile_map.shape[0]
    my_group = lax.axis_index("dp")
    item_ids = jnp.arange(total, dtype=jnp.int32)
    live_all = (item_ids % slot_total < jnp.repeat(trunc_steps, slot_total) - 29).astype(jnp.int32)
    my_slots = my_group * slot_total + jnp.arange(slot_total, dtype=jnp.int32)
    is_mine = tile_map[:, None] == my_slots[None, :]
    dest_source = jnp.sum(jnp.where(is_mine, item_ids[:, None], 0), axis=0)
    every_x, every_cot = (
        lax.all_gather(latents, "dp", axis=0, tiled=True),
        lax.all_gather(cotangent, "dp", axis=0, tiled=True),
    )
    tiles = jnp.take(every_x, dest_source, axis=0)
    cot_tiles = jnp.take(every_cot, dest_source, axis=0)
    slot_times = jnp.take(timesteps, dest_source)
    live_count = jnp.sum(jnp.take(live_all, dest_source))
    placed_grad, weight_parts, gain_local = tile_backward(
        tiles, cot_tiles, slot_times, live_count, gain, w_value, w_gate, w_out
    )
    grad_value, grad_gate, grad_out_proj = (
        lax.psum_scatter(weight_parts[0], "dp", scatter_dimension=0, tiled=True),
        lax.psum_scatter(weight_parts[1], "dp", scatter_dimension=0, tiled=True),
        lax.psum_scatter(weight_parts[2], "dp", scatter_dimension=0, tiled=True),
    )
    grad_gain = lax.psum(gain_local, ("dp", "tensor"))
    return (placed_grad, grad_value, grad_gate, grad_out_proj, grad_gain)


def solution(mesh):
    in_specs = (
        P("dp", "tensor", None),
        P("dp", "tensor", None),
        P(),
        P(),
        P(),
        P(),
        P(None, "tensor"),
        P(None, "tensor"),
        P(None, "tensor"),
    )
    out_specs = (
        P("dp", "tensor", None),
        P("dp", "tensor"),
        P("dp", "tensor"),
        P("dp", "tensor"),
        P(),
    )
    return jax.shard_map(
        per_device, mesh=mesh, in_specs=in_specs, out_specs=out_specs, check_vma=False
    )
```

profile of v0, /device:TPU:0, one launch (start us, length us, event | category | flops | bytes accessed | tf_op | source)
XLA Modules:
  0.0 568.1 jit_solution(17423337908804927241)
XLA Ops:
  10.3 74.4 %all-gather.9.cloned.1.call-done = bf16[88,64,640]{2,1,0:T(8,128)(2,1)} async-done(((bf16[11,64,640]{2,1,0:T(8,128)(2,1)}), bf16[88,64,640]{2,1,0:T(8,128)(2,1)}) %all-gather.9.cloned.1.call-update) | async-done | bytes 7208976 | tf_op jit(solution)/shard_map/all_gather | solution.py:110
  84.7 3.8 gather_fusion.3
  88.4 68.8 %all-gather.5.cloned.1.call-done = bf16[88,64,640]{2,1,0:T(8,128)(2,1)} async-done(((bf16[11,64,640]{2,1,0:T(8,128)(2,1)}), bf16[88,64,640]{2,1,0:T(8,128)(2,1)}) %all-gather.5.cloned.1.call-update) | async-done | bytes 7208976 | tf_op jit(solution)/shard_map/all_gather | solution.py:111
  157.2 3.8 gather_fusion.1
  165.5 43.4 %all-gather.11.cloned.1.call-done = bf16[11,256,640]{2,1,0:T(8,128)(2,1)} async-done(((bf16[11,64,640]{2,1,0:T(8,128)(2,1)}), bf16[11,256,640]{2,1,0:T(8,128)(2,1)}) %all-gather.11.cloned.1.call-update) | async-done | bytes 3604496 | tf_op jit(solution)/shard_map/all_gather | solution.py:33
  208.9 2.7 convert_reduce_fusion
  213.4 45.5 %all-gather.7.cloned.1.call-done = bf16[11,256,640]{2,1,0:T(8,128)(2,1)} async-done(((bf16[11,64,640]{2,1,0:T(8,128)(2,1)}), bf16[11,256,640]{2,1,0:T(8,128)(2,1)}) %all-gather.7.cloned.1.call-update) | async-done | bytes 3604496 | tf_op jit(solution)/shard_map/all_gather | solution.py:34
  258.9 5.0 multiply_convert_fusion.4
  263.9 4.8 fusion.32
  271.3 3.6 broadcast_in_dim.84
  274.9 101.4 %while.16 = (s32[]{:T(128)}, f32[640,640]{1,0:T(8,128)}, f32[640,640]{1,0:T(8,128)}, f32[640,640]{1,0:T(8,128)S(1)}, f32[11,256,640]{2,1,0:T(8,128)}, /*index=5*...) while((s32[]{:T(128)}, f32[640,640]{1,0:T(8,128)}, ...), condition=%wide.region_8.11_spmd, body=%wide.region_7.10_spmd.sunk | while | flops 1684684800 | bytes 56197460 | solution.py:88
  277.1 1.6 fusion.81
  278.6 1.6 multiply_convert_fusion.8
  282.3 2.0 convolution_add_fusion.8
  284.2 1.9 convolution_add_fusion.9
  289.7 1.6 fusion.81
  291.2 1.6 multiply_convert_fusion.8
  294.8 2.0 convolution_add_fusion.8
  296.8 1.9 convolution_add_fusion.9
  302.3 1.6 fusion.81
  303.9 1.6 multiply_convert_fusion.8
  307.5 2.0 convolution_add_fusion.8
  309.5 1.9 convolution_add_fusion.9
  314.9 1.6 fusion.81
  316.5 1.6 multiply_convert_fusion.8
  320.1 2.0 convolution_add_fusion.8
  322.1 1.9 convolution_add_fusion.9
  327.5 1.6 fusion.81
  329.1 1.6 multiply_convert_fusion.8
  332.7 2.0 convolution_add_fusion.8
  334.7 1.9 convolution_add_fusion.9
  340.1 1.6 fusion.81
  341.7 1.6 multiply_convert_fusion.8
  345.3 2.0 convolution_add_fusion.8
  347.3 1.9 convolution_add_fusion.9
  354.3 1.6 multiply_convert_fusion.8
  357.9 2.0 convolution_add_fusion.8
  359.9 1.9 convolution_add_fusion.9
  365.3 1.6 fusion.81
  366.9 1.6 multiply_convert_fusion.8
  370.5 2.0 convolution_add_fusion.8
  372.5 1.9 convolution_add_fusion.9
  380.2 72.1 %reduce-scatter.5.cloned.1.call-done = f32[11,64,640]{2,1,0:T(8,128)} async-done(((f32[11,256,640]{2,1,0:T(8,128)}), f32[11,64,640]{2,1,0:T(8,128)}) %reduce-scatter.5.cloned.1.call-update) | async-done | bytes 1802256 | tf_op jit(solution)/shard_map/reduce_scatter | solution.py:94
  452.4 2.8 multiply_reduce_fusion
  455.2 39.6 %psum.7 = f32[640]{0:T(1024)} all-reduce(f32[640]{0:T(1024)S(1)} %get-tuple-element.72), channel_id=1, replica_groups=mesh['dp'=8,'tensor'=4] {'dp','tensor'}, use_global_device_ids=true, to_apply=%region_16.19 | all-reduce | flops 640 | bytes 5120 | tf_op jit(solution)/shard_map/psum | solution.py:125
  494.8 3.3 select_convert_fusion
  498.1 27.6 %reduce-scatter.9.cloned.1.call-done = f32[80,640]{1,0:T(8,128)} async-done(((f32[640,640]{1,0:T(8,128)}), f32[80,640]{1,0:T(8,128)}) %reduce-scatter.9.cloned.1.call-update) | async-done | bytes 204816 | tf_op jit(solution)/shard_map/reduce_scatter | solution.py:122
  525.6 35.6 %reduce-scatter.11.cloned.1.call-done = f32[80,640]{1,0:T(8,128)} async-done(((f32[640,640]{1,0:T(8,128)}), f32[80,640]{1,0:T(8,128)}) %reduce-scatter.11.cloned.1.call-update) | async-done | bytes 204816 | tf_op jit(solution)/shard_map/reduce_scatter | solution.py:123
  (181 shorter events, 57.0 us)
Async XLA Ops:
  7.2 77.5 %all-gather.9.cloned.1.call-start = ((), (), s32[]{:S(2)}) async-start(), calls=%async_computation.6 | async-start | bytes 8110080 | tf_op jit(solution)/shard_map/all_gather | solution.py:110
  7.9 149.3 %all-gather.5.cloned.1.call-start = ((), (), s32[]{:S(2)}) async-start(), calls=%async_computation.4 | async-start | bytes 8110080 | tf_op jit(solution)/shard_map/all_gather | solution.py:111
  8.7 200.2 %all-gather.11.cloned.1.call-start = ((), (), s32[]{:S(2)}) async-start(), calls=%async_computation.7 | async-start | bytes 4505600 | tf_op jit(solution)/shard_map/all_gather | solution.py:33
  88.4 74.7 %copy-start.13 = (s32[8]{0:T(128)S(1)}, s32[8]{0:T(128)}, u32[]{:S(2)}) copy-start(s32[8]{0:T(128)} %param.17) | copy-start | bytes 100
  162.5 96.4 %all-gather.7.cloned.1.call-start = ((), (), s32[]{:S(2)}) async-start(), calls=%async_computation.5 | async-start | bytes 4505600 | tf_op jit(solution)/shard_map/all_gather | solution.py:34
  163.1 289.3 %reduce-scatter.5.cloned.1.call-start = ((), (), s32[]{:S(2)}) async-start(), calls=%async_computation.8 | async-start | bytes 9011200 | tf_op jit(solution)/shard_map/reduce_scatter | solution.py:94
  213.4 50.5 %copy-start.12 = (f32[640]{0:T(1024)S(1)}, f32[640]{0:T(1024)}, u32[]{:S(2)}) copy-start(f32[640]{0:T(1024)} %param.20) | copy-start | bytes 7684
  258.9 5.0 copy-start.9
  271.3 3.6 copy-start.1
  271.3 3.6 copy-start.2
  277.1 3.6 copy-start.6
  278.6 3.6 copy-start.4
  282.2 3.9 copy-start.7
  284.2 3.3 copy-start.5
  289.6 3.6 copy-start.6
  291.2 3.6 copy-start.4
  294.8 3.9 copy-start.7
  296.8 3.4 copy-start.5
  300.8 3.1 copy-start.10
  302.3 3.6 copy-start.6
  303.9 3.6 copy-start.4
  307.5 3.9 copy-start.7
  309.4 3.4 copy-start.5
  314.9 3.6 copy-start.6
  316.5 3.6 copy-start.4
  320.1 3.9 copy-start.7
  322.1 3.3 copy-start.5
  326.0 3.1 copy-start.10
  327.5 3.6 copy-start.6
  329.1 3.6 copy-start.4
  332.7 3.9 copy-start.7
  334.7 3.3 copy-start.5
  340.1 3.6 copy-start.6
  341.7 3.6 copy-start.4
  345.3 3.9 copy-start.7
  347.3 3.3 copy-start.5
  352.7 3.6 copy-start.6
  354.3 3.6 copy-start.4
  357.9 3.9 copy-start.7
  359.9 3.3 copy-start.5
  365.3 3.6 copy-start.6
  366.9 3.6 copy-start.4
  370.5 3.9 copy-start.7
  372.5 3.3 copy-start.5
  377.5 120.5 %reduce-scatter.7.cloned.1.call-start = ((), (), s32[]{:S(2)}) async-start(), calls=%async_computation.9 | async-start | bytes 1843200 | tf_op jit(solution)/shard_map/reduce_scatter | solution.py:121
  378.1 147.5 %reduce-scatter.9.cloned.1.call-start = ((), (), s32[]{:S(2)}) async-start(), calls=%async_computation.10 | async-start | bytes 1843200 | tf_op jit(solution)/shard_map/reduce_scatter | solution.py:122
  378.8 182.4 %reduce-scatter.11.cloned.1.call-start = ((), (), s32[]{:S(2)}) async-start(), calls=%async_computation.11 | async-start | bytes 1843200 | tf_op jit(solution)/shard_map/reduce_scatter | solution.py:123
  452.4 42.4 %copy-start.11 = (f32[11,64,640]{2,1,0:T(8,128)S(1)}, f32[11,64,640]{2,1,0:T(8,128)}, u32[]{:S(2)}) copy-start(f32[11,64,640]{2,1,0:T(8,128)} %reduce-scatter.5.cloned.1.call-done) | copy-start | bytes 5406724
  (9 other events, 25.3 us)
Sparse Core Ops, SparseCore 0:
  9.6 74.9 all-gather.8
  86.3 70.8 all-gather.4
  162.6 46.2 all-gather.10
  211.2 47.6 all-gather.6
  376.5 75.8 reduce-scatter.4
  455.1 34.5 reduce-scatter.6
  492.5 33.0 reduce-scatter.8
  528.5 32.6 reduce-scatter.10
where the time goes:
time: 570 us; the launch traced here: 568 us
  waiting for transfers between devices  371 us (65%)
  matrix products  95 us (17%)
  blocking collectives  39.6 us (7%)
  other arithmetic  24.2 us (4%)
  local copies, waits for them, and re-layouts  17.3 us (3%)
  between operations  14.3 us (3%)
  loops' own time  6.18 us (1%)
    all_gather x1, waiting for transfers between devices, per_device(): lax.all_gather(latents, 'dp', axis=0, tiled=True)  74.4 us
    reduce_scatter x1, waiting for transfers between devices, tile_backward(): lax.psum_scatter(normed_buf, 'tensor', scatter_dimension=1, tiled=True)  72.1 us
    all_gather x1, waiting for transfers between devices, per_device(): lax.all_gather(cotangent, 'dp', axis=0, tiled=True)  68.8 us
    all_gather x1, waiting for transfers between devices, tile_backward(): lax.all_gather(cot_tiles, 'tensor', axis=1, tiled=True)  45.5 us
    all_gather x1, waiting for transfers between devices, tile_backward(): lax.all_gather(tiles, 'tensor', axis=1, tiled=True)  43.4 us
    psum x1, blocking collectives, per_device(): grad_gain = lax.psum(gain_local, ('dp', 'tensor'))  39.6 us
    reduce_scatter x1, waiting for transfers between devices, per_device(): lax.psum_scatter(weight_parts[2], 'dp', scatter_dimension=0, tiled=True)  35.6 us
    reduce_scatter x1, waiting for transfers between devices, per_device(): lax.psum_scatter(weight_parts[1], 'dp', scatter_dimension=0, tiled=True)  27.6 us
  transfers between devices with their start and end apart: 8, of which 7 were waited for; matrix products, arithmetic and copies ran while one was open for 3% of the time, Pallas kernels for 0%

commit v1 on v0

--- a/solution.py
+++ b/solution.py
@@ -4,6 +4,11 @@
 from jax.sharding import PartitionSpec as P
 
 eps = 1e-05
+
+
+def add_all(block, axis):
+    parts = lax.all_gather(block, axis)
+    return jnp.sum(parts, axis=0)
 
 
 def alpha_bars():
@@ -122,7 +127,7 @@
         lax.psum_scatter(weight_parts[1], "dp", scatter_dimension=0, tiled=True),
         lax.psum_scatter(weight_parts[2], "dp", scatter_dimension=0, tiled=True),
     )
-    grad_gain = lax.psum(gain_local, ("dp", "tensor"))
+    grad_gain = add_all(gain_local, ("dp", "tensor"))
     return (placed_grad, grad_value, grad_gate, grad_out_proj, grad_gain)
 
 

time: 570 us -> 570 us (level)
  waiting for transfers between devices: 371 us -> 343 us
  blocking collectives: 39.6 us -> 67.4 us
    all_gather x0 -> x1, blocking collectives: none -> 67.4 us  [add_all(): parts = lax.all_gather(block, axis)]
    psum x1 -> x0, blocking collectives: 39.6 us -> none  [per_device(): grad_gain = lax.psum(gain_local, ('dp', 'tensor'))]
    reduce_scatter x1, waiting for transfers between devices: 27.6 us -> 0.01 us  [per_device(): lax.psum_scatter(weight_parts[1], 'dp', scatter_dimension=0, tiled=True)]
  transfers between devices with their start and end apart: 8 -> 8, of which waited for: 7 -> 6; matrix products, arithmetic and copies ran while one was open for 3% -> 3% of each run, Pallas kernels for 0% -> 0%
where the time goes in v1:
time: 570 us; the launch traced here: 568 us
  waiting for transfers between devices  343 us (60%)
  matrix products  95 us (17%)
  blocking collectives  67.4 us (12%)
  other arithmetic  24.9 us (4%)
  local copies, waits for them, and re-layouts  17.3 us (3%)
  between operations  14.3 us (3%)
  loops' own time  6.18 us (1%)
    all_gather x1, waiting for transfers between devices, per_device(): lax.all_gather(latents, 'dp', axis=0, tiled=True)  74.4 us
    reduce_scatter x1, waiting for transfers between devices, tile_backward(): lax.psum_scatter(normed_buf, 'tensor', scatter_dimension=1, tiled=True)  72.1 us
    all_gather x1, waiting for transfers between devices, per_device(): lax.all_gather(cotangent, 'dp', axis=0, tiled=True)  68.8 us
    all_gather x1, blocking collectives, add_all(): parts = lax.all_gather(block, axis)  67.4 us
    all_gather x1, waiting for transfers between devices, tile_backward(): lax.all_gather(cot_tiles, 'tensor', axis=1, tiled=True)  45.5 us
    all_gather x1, waiting for transfers between devices, tile_backward(): lax.all_gather(tiles, 'tensor', axis=1, tiled=True)  43.4 us
    reduce_scatter x1, waiting for transfers between devices, per_device(): lax.psum_scatter(weight_parts[2], 'dp', scatter_dimension=0, tiled=True)  34.5 us
    dot_general x8, matrix products, one_slot(): lax.dot_general(norm_tile, d_gate, first_dims, preferred_element_type=jnp...  15.7 us
  transfers between devices with their start and end apart: 8, of which 6 were waited for; matrix products, arithmetic and copies ran while one was open for 3% of the time, Pallas kernels for 0%

profile of v1, /device:TPU:0, one launch (start us, length us, event | category | flops | bytes accessed | tf_op | source)
XLA Modules:
  0.0 567.9 jit_solution(8179840159577173374)
XLA Ops:
  10.3 74.4 %all-gather.11.cloned.1.call-done = bf16[88,64,640]{2,1,0:T(8,128)(2,1)} async-done(((bf16[11,64,640]{2,1,0:T(8,128)(2,1)}), bf16[88,64,640]{2,1,0:T(8,128)(2,1)}) %all-gather.11.cloned.1.call-update) | async-done | bytes 7208976 | tf_op jit(solution)/shard_map/all_gather | solution.py:115
  84.7 3.8 gather_fusion.3
  88.4 68.8 %all-gather.7.cloned.1.call-done = bf16[88,64,640]{2,1,0:T(8,128)(2,1)} async-done(((bf16[11,64,640]{2,1,0:T(8,128)(2,1)}), bf16[88,64,640]{2,1,0:T(8,128)(2,1)}) %all-gather.7.cloned.1.call-update) | async-done | bytes 7208976 | tf_op jit(solution)/shard_map/all_gather | solution.py:116
  157.2 3.8 gather_fusion.1
  165.5 43.4 %all-gather.13.cloned.1.call-done = bf16[11,256,640]{2,1,0:T(8,128)(2,1)} async-done(((bf16[11,64,640]{2,1,0:T(8,128)(2,1)}), bf16[11,256,640]{2,1,0:T(8,128)(2,1)}) %all-gather.13.cloned.1.call-update) | async-done | bytes 3604496 | tf_op jit(solution)/shard_map/all_gather | solution.py:38
  208.9 2.7 convert_reduce_fusion
  213.4 45.5 %all-gather.9.cloned.1.call-done = bf16[11,256,640]{2,1,0:T(8,128)(2,1)} async-done(((bf16[11,64,640]{2,1,0:T(8,128)(2,1)}), bf16[11,256,640]{2,1,0:T(8,128)(2,1)}) %all-gather.9.cloned.1.call-update) | async-done | bytes 3604496 | tf_op jit(solution)/shard_map/all_gather | solution.py:39
  258.9 5.0 multiply_convert_fusion.4
  263.9 4.8 fusion.32
  271.3 3.6 broadcast_in_dim.84
  274.9 101.4 %while.16 = (s32[]{:T(128)}, f32[640,640]{1,0:T(8,128)}, f32[640,640]{1,0:T(8,128)}, f32[640,640]{1,0:T(8,128)S(1)}, f32[11,256,640]{2,1,0:T(8,128)}, /*index=5*...) while((s32[]{:T(128)}, f32[640,640]{1,0:T(8,128)}, ...), condition=%wide.region_8.11_spmd, body=%wide.region_7.10_spmd.sunk | while | flops 1684684800 | bytes 56197460 | solution.py:93
  277.1 1.6 fusion.81
  278.6 1.6 multiply_convert_fusion.8
  282.3 2.0 convolution_add_fusion.8
  284.2 1.9 convolution_add_fusion.9
  289.7 1.6 fusion.81
  291.2 1.6 multiply_convert_fusion.8
  294.8 2.0 convolution_add_fusion.8
  296.8 1.9 convolution_add_fusion.9
  302.3 1.6 fusion.81
  303.9 1.6 multiply_convert_fusion.8
  307.5 2.0 convolution_add_fusion.8
  309.5 1.9 convolution_add_fusion.9
  314.9 1.6 fusion.81
  316.5 1.6 multiply_convert_fusion.8
  320.1 2.0 convolution_add_fusion.8
  322.1 1.9 convolution_add_fusion.9
  327.5 1.6 fusion.81
  329.1 1.6 multiply_convert_fusion.8
  332.7 2.0 convolution_add_fusion.8
  334.7 1.9 convolution_add_fusion.9
  340.1 1.6 fusion.81
  341.7 1.6 multiply_convert_fusion.8
  345.3 2.0 convolution_add_fusion.8
  347.3 1.9 convolution_add_fusion.9
  352.7 1.6 fusion.81
  354.3 1.6 multiply_convert_fusion.8
  357.9 2.0 convolution_add_fusion.8
  359.9 1.9 convolution_add_fusion.9
  365.3 1.6 fusion.81
  366.9 1.6 multiply_convert_fusion.8
  370.5 2.0 convolution_add_fusion.8
  372.5 1.9 convolution_add_fusion.9
  380.2 72.1 %reduce-scatter.5.cloned.1.call-done = f32[11,64,640]{2,1,0:T(8,128)} async-done(((f32[11,256,640]{2,1,0:T(8,128)}), f32[11,64,640]{2,1,0:T(8,128)}) %reduce-scatter.5.cloned.1.call-update) | async-done | bytes 1802256 | tf_op jit(solution)/shard_map/reduce_scatter | solution.py:99
  452.4 2.8 multiply_reduce_fusion
  455.2 67.4 %all-gather.1 = f32[32,1,640]{2,1,0:T(1,128)S(1)} all-gather(f32[1,1,640]{2,1,0:T(1,128)S(1)} %reshape.133), channel_id=2, replica_groups=mesh['dp'=8,'tensor'=4] {'dp','tensor'}, dimensions={0}, use_global_device_ids=true | all-gather | bytes 84480 | tf_op jit(solution)/shard_map/all_gather | solution.py:10
  523.2 3.3 select_convert_fusion
  526.5 34.5 %reduce-scatter.11.cloned.1.call-done = f32[80,640]{1,0:T(8,128)} async-done(((f32[640,640]{1,0:T(8,128)}), f32[80,640]{1,0:T(8,128)}) %reduce-scatter.11.cloned.1.call-update) | async-done | bytes 204816 | tf_op jit(solution)/shard_map/reduce_scatter | solution.py:128
  (183 shorter events, 56.1 us)
Async XLA Ops:
  7.2 77.5 %all-gather.11.cloned.1.call-start = ((), (), s32[]{:S(2)}) async-start(), calls=%async_computation.6 | async-start | bytes 8110080 | tf_op jit(solution)/shard_map/all_gather | solution.py:115
  7.9 149.3 %all-gather.7.cloned.1.call-start = ((), (), s32[]{:S(2)}) async-start(), calls=%async_computation.4 | async-start | bytes 8110080 | tf_op jit(solution)/shard_map/all_gather | solution.py:116
  8.7 200.2 %all-gather.13.cloned.1.call-start = ((), (), s32[]{:S(2)}) async-start(), calls=%async_computation.7 | async-start | bytes 4505600 | tf_op jit(solution)/shard_map/all_gather | solution.py:38
  88.4 74.7 %copy-start.13 = (s32[8]{0:T(128)S(1)}, s32[8]{0:T(128)}, u32[]{:S(2)}) copy-start(s32[8]{0:T(128)} %param.17) | copy-start | bytes 100
  162.5 96.4 %all-gather.9.cloned.1.call-start = ((), (), s32[]{:S(2)}) async-start(), calls=%async_computation.5 | async-start | bytes 4505600 | tf_op jit(solution)/shard_map/all_gather | solution.py:39
  163.1 289.3 %reduce-scatter.5.cloned.1.call-start = ((), (), s32[]{:S(2)}) async-start(), calls=%async_computation.8 | async-start | bytes 9011200 | tf_op jit(solution)/shard_map/reduce_scatter | solution.py:99
  213.4 50.5 %copy-start.12 = (f32[640]{0:T(1024)S(1)}, f32[640]{0:T(1024)}, u32[]{:S(2)}) copy-start(f32[640]{0:T(1024)} %param.20) | copy-start | bytes 7684
  258.9 5.0 copy-start.9
  271.3 3.6 copy-start.1
  271.3 3.6 copy-start.2
  277.1 3.6 copy-start.6
  278.6 3.6 copy-start.4
  282.2 3.9 copy-start.7
  284.2 3.3 copy-start.5
  289.6 3.6 copy-start.6
  291.2 3.6 copy-start.4
  294.8 3.9 copy-start.7
  296.8 3.4 copy-start.5
  300.8 3.1 copy-start.10
  302.3 3.6 copy-start.6
  303.9 3.6 copy-start.4
  307.5 3.9 copy-start.7
  309.4 3.4 copy-start.5
  314.9 3.6 copy-start.6
  316.5 3.6 copy-start.4
  320.1 3.9 copy-start.7
  322.1 3.3 copy-start.5
  326.0 3.1 copy-start.10
  327.5 3.6 copy-start.6
  329.1 3.6 copy-start.4
  332.7 3.9 copy-start.7
  334.7 3.3 copy-start.5
  340.1 3.6 copy-start.6
  341.7 3.6 copy-start.4
  345.3 3.9 copy-start.7
  347.3 3.3 copy-start.5
  352.7 3.6 copy-start.6
  354.3 3.6 copy-start.4
  357.9 3.9 copy-start.7
  359.9 3.3 copy-start.5
  365.3 3.6 copy-start.6
  366.9 3.6 copy-start.4
  370.5 3.9 copy-start.7
  372.5 3.3 copy-start.5
  377.5 149.0 %reduce-scatter.7.cloned.1.call-start = ((), (), s32[]{:S(2)}) async-start(), calls=%async_computation.9 | async-start | bytes 1843200 | tf_op jit(solution)/shard_map/reduce_scatter | solution.py:126
  378.1 148.5 %reduce-scatter.9.cloned.1.call-start = ((), (), s32[]{:S(2)}) async-start(), calls=%async_computation.10 | async-start | bytes 1843200 | tf_op jit(solution)/shard_map/reduce_scatter | solution.py:127
  378.8 182.2 %reduce-scatter.11.cloned.1.call-start = ((), (), s32[]{:S(2)}) async-start(), calls=%async_computation.11 | async-start | bytes 1843200 | tf_op jit(solution)/shard_map/reduce_scatter | solution.py:128
  452.4 70.8 %copy-start.11 = (f32[11,64,640]{2,1,0:T(8,128)S(1)}, f32[11,64,640]{2,1,0:T(8,128)}, u32[]{:S(2)}) copy-start(f32[11,64,640]{2,1,0:T(8,128)} %reduce-scatter.5.cloned.1.call-done) | copy-start | bytes 5406724
  (9 other events, 25.3 us)
Sparse Core Ops, SparseCore 0:
  9.6 74.9 all-gather.10
  86.3 70.8 all-gather.6
  162.6 46.2 all-gather.12
  211.2 47.6 all-gather.8
  376.5 75.8 reduce-scatter.4
  455.1 34.5 reduce-scatter.6
  492.6 32.7 reduce-scatter.8
  528.2 32.8 reduce-scatter.10
